TPU v7x, 128 devices: a whole 4x4x4 slice. The times are simulated.
128 devices in a mesh: tm: 8 (over x, core), batch: 16 (over z, y).
Axes of the slice: x: 4, y: 4, z: 4, core: 2. Of those that a mesh axis runs over, the one named last changes fastest.
Arguments:
- latents: float32 [8, 32, 4096], P('tm', None, 'batch'), may hold values from -6 to 6
- shifts: int32 [32], replicated, may hold values from 0 to 7
- starts: int32 [32], replicated, may hold values from 0 to 2
- labels: int32 [32], replicated, may hold values from 0 to 1000
- class_table: bfloat16 [1001, 1152], replicated, may hold values from -6 to 6
- w_freq: bfloat16 [256, 1152], replicated, may hold values from -0.375 to 0.375
- w_time: bfloat16 [1152, 1152], replicated, may hold values from -0.1875 to 0.1875
- w_ada: bfloat16 [1152, 9216], P(None, 'tm'), may hold values from -0.1875 to 0.1875
- w_patch: bfloat16 [16, 1152], replicated, may hold values from -1.5 to 1.5
- w_qkv: bfloat16 [1152, 3456], P('batch', 'tm'), may hold values from -1 to 1
- w_proj: bfloat16 [1152, 1152], P('tm', 'batch'), may hold values from -0.1875 to 0.1875
- w_fc1: bfloat16 [1152, 4608], P('batch', 'tm'), may hold values from -0.1875 to 0.1875
- w_fc2: bfloat16 [4608, 1152], P('tm', 'batch'), may hold values from -0.09375 to 0.09375
- w_final: bfloat16 [1152, 16], replicated, may hold values from -0.1875 to 0.1875
Outputs:
- new_latents: float32 [8, 32, 4096], P('tm', None, 'batch')
- velocity: bfloat16 [8, 32, 4096], P('tm', None, 'batch')
All inputs are finite; a program needn't handle non-finite values.
Results may differ from a plain program's by a relative error of at most 0.0091.
Values may be sent and summed in bfloat16 or wider, within the bound.
A program may use at most 128 MiB of HBM per device.

v0:
```python
import math

import jax
import jax.numpy as jnp
from jax import lax
from jax.sharding import PartitionSpec as P

D = 1152
HEADS = 16
FREQ = 256
GRID = 16
STEPS = 18


def in_order(parts, dim):
    lengths = list(parts.shape[1:])
    lengths[dim] *= parts.shape[0]
    return jnp.moveaxis(parts, 0, dim).reshape(lengths)


def from_everyone(array, axis):
    copies = jnp.broadcast_to(array, (lax.axis_size(axis), *array.shape))
    return lax.all_to_all(copies, axis, split_axis=0, concat_axis=0, tiled=True)


def gathered_copies(array, axis, dim):
    return in_order(from_everyone(array, axis), dim)


def gather_packed(arrays, axis, dims):
    line = jnp.concatenate([a.reshape(-1) for a in arrays])
    lines, at, gathered = (lax.all_gather(line, axis), 0, [])
    for a, dim in zip(arrays, dims):
        parts = lines[:, at : at + a.size].reshape(-1, *a.shape)
        gathered.append(in_order(parts, dim))
        at += a.size
    return tuple(gathered)


def gather_turned(arrays, axis, dims):
    turned = [jnp.moveaxis(a, dim, 0) for a, dim in zip(arrays, dims)]
    both = jnp.concatenate([t.reshape(len(t), -1) for t in turned], axis=1)
    whole, at, gathered = (lax.all_gather(both, axis, axis=0, tiled=True), 0, [])
    for t, dim in zip(turned, dims):
        slab = whole[:, at : at + t[0].size].reshape(-1, *t.shape[1:])
        gathered.append(jnp.moveaxis(slab, 0, dim))
        at += t[0].size
    return tuple(gathered)


def layer_norm(values):
    average = jnp.mean(values, axis=-1, keepdims=True)
    centred = values - average
    variance = jnp.mean(centred * centred, axis=-1, keepdims=True)
    return centred * lax.rsqrt(variance + 1e-06)


def position_table(token_count):
    token_ids = jnp.arange(token_count, dtype=jnp.int32)
    row_ids = (token_ids // GRID).astype(jnp.float32)
    col_ids = (token_ids % GRID).astype(jnp.float32)
    quarter = D // 4
    omegas = jnp.exp(-math.log(10000.0) * jnp.arange(quarter, dtype=jnp.float32) / quarter)
    col_angle = col_ids[:, None] * omegas[None, :]
    row_angle = row_ids[:, None] * omegas[None, :]
    return jnp.concatenate(
        [jnp.sin(col_angle), jnp.cos(col_angle), jnp.sin(row_angle), jnp.cos(row_angle)], axis=1
    )


def cond_activation(step_ids, class_ids, class_table, w_freq, w_time):
    half_freq = FREQ // 2
    freqs = jnp.exp(-math.log(10000.0) * jnp.arange(half_freq, dtype=jnp.float32) / half_freq)
    tvalue = 1000.0 * (1.0 - step_ids.astype(jnp.float32) / STEPS)
    angles = tvalue[:, None] * freqs[None, :]
    embedded = jnp.concatenate([jnp.cos(angles), jnp.sin(angles)], axis=1).astype(jnp.bfloat16)
    hidden_time = jax.nn.silu(jnp.dot(embedded, w_freq, preferred_element_type=jnp.float32)).astype(
        jnp.bfloat16
    )
    condition = jnp.dot(hidden_time, w_time, preferred_element_type=jnp.float32) + jnp.take(
        class_table, class_ids, axis=0
    ).astype(jnp.float32)
    return jax.nn.silu(condition).astype(jnp.bfloat16)


def attend(qkv_rows, point_count, head_count):
    token_count = qkv_rows.shape[0] // point_count
    head_size = qkv_rows.shape[1] // (3 * head_count)
    grouped = qkv_rows.reshape(point_count, token_count, head_count, 3, head_size)

    def one_point(block):
        query = block[:, :, 0, :]
        keys = block[:, :, 1, :]
        values = block[:, :, 2, :]
        scores = jnp.einsum("qhd,khd->hqk", query, keys, preferred_element_type=jnp.float32) * (
            1.0 / math.sqrt(head_size)
        )
        peak = jnp.max(scores, axis=-1, keepdims=True)
        weights = jnp.exp(scores - peak)
        weights = (weights / jnp.sum(weights, axis=-1, keepdims=True)).astype(jnp.bfloat16)
        attended = jnp.einsum("hqk,khd->qhd", weights, values, preferred_element_type=jnp.float32)
        return attended.astype(jnp.bfloat16).reshape(token_count, head_count * head_size)

    return lax.map(one_point, grouped).reshape(point_count * token_count, head_count * head_size)


def forward(patch_rows, modulation, w_patch, w_final, attention_fn, mlp_fn):
    point_count, lat_count = patch_rows.shape
    patch_size = w_patch.shape[0]
    model_width = w_patch.shape[1]
    token_count = lat_count // patch_size
    tokens = jnp.dot(
        patch_rows.reshape(point_count * token_count, patch_size),
        w_patch,
        preferred_element_type=jnp.float32,
    )
    tokens = (
        tokens.reshape(point_count, token_count, model_width) + position_table(token_count)[None]
    )
    mod_float = modulation.astype(jnp.float32)[:, None, :]
    mod_parts = [
        mod_float[:, :, block_index * model_width : (block_index + 1) * model_width]
        for block_index in range(8)
    ]
    normed = (
        (layer_norm(tokens) * (1.0 + mod_parts[1]) + mod_parts[0])
        .astype(jnp.bfloat16)
        .reshape(-1, model_width)
    )
    mixed = tokens + mod_parts[2] * attention_fn(normed).reshape(
        point_count, token_count, model_width
    )
    normed_two = (
        (layer_norm(mixed) * (1.0 + mod_parts[4]) + mod_parts[3])
        .astype(jnp.bfloat16)
        .reshape(-1, model_width)
    )
    residual = mixed + mod_parts[5] * mlp_fn(normed_two).reshape(
        point_count, token_count, model_width
    )
    final_in = (
        (layer_norm(residual) * (1.0 + mod_parts[7]) + mod_parts[6])
        .astype(jnp.bfloat16)
        .reshape(-1, model_width)
    )
    return (
        jnp.dot(final_in, w_final, preferred_element_type=jnp.float32)
        .astype(jnp.bfloat16)
        .reshape(point_count, lat_count)
    )


def local(
    latents,
    shifts,
    starts,
    labels,
    class_table,
    w_freq,
    w_time,
    w_ada,
    w_patch,
    w_qkv,
    w_proj,
    w_fc1,
    w_fc2,
    w_final,
):
    tm_count = lax.axis_size("tm")
    tm_index = lax.axis_index("tm")
    batch_index = lax.axis_index("batch")
    local_steps = latents.shape[0]
    window = local_steps * tm_count
    whole = gathered_copies(latents, "tm", 0)
    local_positions = tm_index * local_steps + jnp.arange(local_steps, dtype=jnp.int32)[:, None]
    source_rows = jnp.minimum(local_positions + shifts[None, :], window - 1)
    points = jnp.take_along_axis(whole, source_rows[:, :, None], axis=0)
    anchor = jnp.take_along_axis(whole, shifts[None, :, None], axis=0)[0]
    by_sample = lax.all_to_all(
        points.astype(jnp.bfloat16), "batch", split_axis=1, concat_axis=2, tiled=True
    )
    sample_count = by_sample.shape[1]
    lat_count = by_sample.shape[2]
    own_shifts = lax.dynamic_slice_in_dim(shifts, batch_index * sample_count, sample_count)
    own_starts = lax.dynamic_slice_in_dim(starts, batch_index * sample_count, sample_count)
    own_labels = lax.dynamic_slice_in_dim(labels, batch_index * sample_count, sample_count)
    window_positions = jnp.arange(window, dtype=jnp.int32)[:, None]
    step_ids = (own_starts + own_shifts)[None, :] + window_positions
    class_ids = jnp.broadcast_to(own_labels[None, :], step_ids.shape)
    activation = cond_activation(
        step_ids.reshape(-1), class_ids.reshape(-1), class_table, w_freq, w_time
    )
    own_columns = jnp.dot(activation, w_ada, preferred_element_type=jnp.float32).astype(
        jnp.bfloat16
    )
    modulation = lax.all_to_all(own_columns, "tm", split_axis=0, concat_axis=1, tiled=True)
    point_rows = by_sample.reshape(local_steps * sample_count, lat_count)
    point_count = point_rows.shape[0]
    pieces = gather_packed((w_qkv, w_proj, w_fc1, w_fc2), "tm", (1, 0, 1, 0))
    qkv_full, proj_full, fc1_full, fc2_full = gather_turned(
        (pieces[0], pieces[1], pieces[2], pieces[3]), "batch", (0, 1, 0, 1)
    )

    def attention_fn(normed):
        qkv_rows = jnp.dot(normed, qkv_full, preferred_element_type=jnp.float32).astype(
            jnp.bfloat16
        )
        attended = attend(qkv_rows, point_count, HEADS)
        return jnp.dot(attended, proj_full, preferred_element_type=jnp.float32)

    def mlp_fn(normed_two):
        hidden_units = jax.nn.gelu(
            jnp.dot(normed_two, fc1_full, preferred_element_type=jnp.float32), approximate=True
        ).astype(jnp.bfloat16)
        return jnp.dot(hidden_units, fc2_full, preferred_element_type=jnp.float32)

    velocity_mid = forward(point_rows, modulation, w_patch, w_final, attention_fn, mlp_fn)
    velocity_mid = velocity_mid.reshape(local_steps, sample_count, lat_count)
    velocity_out = lax.all_to_all(velocity_mid, "batch", split_axis=2, concat_axis=1, tiled=True)
    velocity_float = velocity_out.astype(jnp.float32)
    summed = jnp.cumsum(velocity_float, axis=0)
    running = jnp.concatenate([jnp.zeros_like(summed), summed[:-1]], axis=0)
    block_sum = jnp.sum(velocity_float, axis=0)
    block_sums = gathered_copies(block_sum[None], "tm", 0)
    lower_blocks = jnp.arange(tm_count, dtype=jnp.int32) < tm_index
    earlier_sum = jnp.sum(jnp.where(lower_blocks[:, None, None], block_sums, 0.0), axis=0)
    latents_out = anchor[None] + (earlier_sum[None] + running) * (1.0 / STEPS)
    return (latents_out, velocity_out)


def solution(mesh):
    placed = (
        P("tm", None, "batch"),
        P(),
        P(),
        P(),
        P(),
        P(),
        P(),
        P(None, "tm"),
        P(),
        P("batch", "tm"),
        P("tm", "batch"),
        P("batch", "tm"),
        P("tm", "batch"),
        P(),
    )
    return jax.shard_map(
        local,
        mesh=mesh,
        in_specs=placed,
        out_specs=(P("tm", None, "batch"), P("tm", None, "batch")),
        check_vma=False,
    )
```

profile of v0, /device:TPU:1, one launch (start us, length us, event | category | flops | bytes accessed | tf_op | source)
XLA Modules:
  0.0 392.2 jit_solution(1327249624059637661)
XLA Ops:
  12.8 34.8 %all-gather.7.cloned.1.call-done = bf16[8,1,124416]{2,1,0:T(2,128)(2,1)} async-done(((bf16[1,1,124416]{2,1,0:T(2,128)(2,1)}), bf16[8,1,124416]{2,1,0:T(2,128)(2,1)}) %all-gather.7.cloned.1.call-update) | async-done | bytes 1990672 | tf_op jit(solution)/shard_map/all_gather | solution.py:32
  58.4 3.1 reshape.290
  66.3 3.7 reshape_reshape.11
  80.9 3.7 all-to-all-start.2
  84.7 2.8 multiply_cosine_fusion
  90.0 4.1 %all-to-all-start = ((f32[8,1,32,256]{3,2,1,0:T(8,128)}), f32[8,1,32,256]{3,2,1,0:T(8,128)S(1)}, u32[]{:S(2)}, u32[]{:S(2)}) async-start(f32[8,1,32,256]{3,2,1,0:T(8,128)} %broadcast_in_dim.44), calls=%async_computation | async-start | bytes 524288 | tf_op jit(solution)/shard_map/all_to_all | solution.py:23
  95.4 5.3 %all-to-all-done = f32[8,1,32,256]{3,2,1,0:T(8,128)S(1)} async-done(((f32[8,1,32,256]{3,2,1,0:T(8,128)}), f32[8,1,32,256]{3,2,1,0:T(8,128)S(1)}, u32[]{:S(2)}, u32[]{:S(2)}) %all-to-all-start) | async-done | bytes 262176 | tf_op jit(solution)/shard_map/all_to_all | solution.py:23
  103.3 6.6 %all-to-all-start.1 = ((bf16[16,2,256]{2,1,0:T(2,128)(2,1)}), bf16[16,2,256]{2,1,0:T(2,128)(2,1)S(1)}, u32[]{:S(2)}, u32[]{:S(2)}) async-start(bf16[16,2,256]{2,1,0:T(2,128)(2,1)} %reshape.344), calls=%async_computation.1 | async-start | bytes 32768 | tf_op jit(solution)/shard_map/all_to_all | solution.py:179
  110.6 6.0 %all-to-all-done.1 = bf16[16,2,256]{2,1,0:T(2,128)(2,1)S(1)} async-done(((bf16[16,2,256]{2,1,0:T(2,128)(2,1)}), bf16[16,2,256]{2,1,0:T(2,128)(2,1)S(1)}, u32[]{:S(2)}, u32[]{:S(2)}) %all-to-all-start.1) | async-done | bytes 16416 | tf_op jit(solution)/shard_map/all_to_all | solution.py:179
  119.4 143.0 %all-gather.5.cloned.1.call-done = bf16[1152,13824]{1,0:T(8,128)(2,1)} async-done(((bf16[72,13824]{1,0:T(8,128)(2,1)}), bf16[1152,13824]{1,0:T(8,128)(2,1)}) %all-gather.5.cloned.1.call-update) | async-done | bytes 31850512 | tf_op jit(solution)/shard_map/all_gather | solution.py:43
  262.4 9.5 %fusion.25 = bf16[512,3456]{1,0:T(8,128)(2,1)} fusion(bf16[512,1152]{1,0:T(8,128)(2,1)S(1)} %bitcast.146, bf16[1152,13824]{1,0:T(8,128)(2,1)} %all-gather.5.cloned.1.call-done), kind=kOutput, calls=%fused_computation.33 | convolution fusion | flops 4078632960 | bytes 12681216 | tf_op jit(solution)/shard_map/dot_general | solution.py:205
  271.9 4.4 %copy.85 = bf16[512,3456]{0,1:T(8,128)(2,1)S(1)} copy(bf16[512,3456]{1,0:T(8,128)(2,1)} %fusion.25) | data formatting | bytes 7077888 | tf_op jit(solution)/shard_map/convert_element_type | solution.py:205
  276.3 3.2 reshape.294
  281.9 12.7 %while.10 = (s32[]{:T(128)}, bf16[2,256,1152]{1,2,0:T(8,128)(2,1)}, bf16[2,256,16,3,72]{1,4,2,3,0:T(8,128)(2,1)S(1)}, s32[]{:T(128)}) while((s32[]{:T(128)}, bf16[2,256,1152]{1,2,0:T(8,128)(2,1)}, bf16[2,256,16,3,72]{1,4,2,3,0:T(8,128)(2,1)S(1)}, s32[]{:T(128)}) %tuple.53), condition=%wide.region_5.7_spmd, body=%wide.region_2.6_spmd.sunk | while | flops 308576512 | bytes 33325180 | solution.py:104
  282.8 3.1 fusion.82
  289.2 3.1 fusion.82
  294.7 4.8 %fusion.68 = (f32[2,256]{1,0:T(2,128)S(1)}, f32[2,256,1152]{2,1,0:T(8,128)S(1)}) fusion(f32[2,256,1152]{2,1,0:T(8,128)} %copy-done.2, bf16[2,256,1152]{1,2,0:T(8,128)(2,1)} %get-tuple-element.20, bf16[1152,13824]{1,0:T(8,128)(2,1)} %all-gather.5.cloned.1.call-done, f32[2,1152]{1,0:T(2,128)} %get-tuple-element.60), kind=kOutput, calls=%fused_computation.135 | convolution fusion | flops 1360723456 | bytes 8563712 | tf_op jit(solution)/shard_map/dot_general | solution.py:209
  300.7 18.6 %fusion.9 = f32[512,1152]{1,0:T(8,128)} fusion(bf16[1152,13824]{1,0:T(8,128)(2,1)} %all-gather.5.cloned.1.call-done, bf16[512,1152]{1,0:T(8,128)(2,1)S(1)} %bitcast.147), kind=kOutput, calls=%fused_computation.19 | convolution fusion | flops 10892869632 | bytes 24772608 | tf_op jit(solution)/shard_map/dot_general | solution.py:215
  326.0 22.6 %reduce.3 = bf16[4096,2]{1,0:T(8,128)(2,1)S(1)} reduce(bf16[4096,1,2]{2,1,0:T(2,128)(2,1)S(1)} %bitcast.134, bf16[]{:T(256)} %broadcast.339), dimensions={1}, to_apply=%bitcast.103.reduce_sub_computation | reduce | bytes 32770
  350.2 11.2 %all_to_all.56 = bf16[16,2,256]{2,1,0:T(2,128)(2,1)S(1)} all-to-all(bf16[16,2,256]{2,1,0:T(2,128)(2,1)S(1)} %reshape.346), channel_id=1, replica_groups=mesh['tm'=8,'batch'=16] {'batch'}, dimensions={0} | all-to-all | bytes 32768 | tf_op jit(solution)/shard_map/all_to_all | solution.py:219
  361.5 4.4 %reshape.347 = bf16[4096,1,2]{2,1,0:T(2,128)(2,1)} reshape(bf16[16,2,256]{2,1,0:T(2,128)(2,1)S(1)} %all_to_all.56) | data formatting | bytes 32768
  365.8 4.5 %copy.90 = bf16[1,2,4096]{2,1,0:T(2,128)(2,1)S(1)} copy(bf16[1,2,4096]{1,0,2:T(2,128)(2,1)} %bitcast.135) | data formatting | bytes 32768 | tf_op jit(solution)/shard_map/all_to_all | solution.py:219
  371.2 6.5 %all-to-all-start.4 = ((f32[8,1,32,256]{3,2,1,0:T(8,128)}), f32[8,1,32,256]{3,2,1,0:T(8,128)S(1)}, u32[]{:S(2)}, u32[]{:S(2)}) async-start(f32[8,1,32,256]{3,2,1,0:T(8,128)} %broadcast_in_dim.85), calls=%async_computation.4 | async-start | bytes 524288 | tf_op jit(solution)/shard_map/all_to_all | solution.py:23
  379.1 5.1 %all-to-all-done.4 = f32[8,1,32,256]{3,2,1,0:T(8,128)S(1)} async-done(((f32[8,1,32,256]{3,2,1,0:T(8,128)}), f32[8,1,32,256]{3,2,1,0:T(8,128)S(1)}, u32[]{:S(2)}, u32[]{:S(2)}) %all-to-all-start.4) | async-done | bytes 262176 | tf_op jit(solution)/shard_map/all_to_all | solution.py:23
  (149 shorter events, 63.0 us)
Async XLA Ops:
  7.2 70.5 %copy-start = (bf16[1152,1152]{1,0:T(8,128)(2,1)S(1)}, bf16[1152,1152]{1,0:T(8,128)(2,1)}, u32[]{:S(2)}) copy-start(bf16[1152,1152]{1,0:T(8,128)(2,1)} %param.25) | copy-start | bytes 7962628
  7.2 40.5 %all-gather.7.cloned.1.call-start = ((), (), s32[]{:S(2)}) async-start(), calls=%async_computation.6 | async-start | bytes 4478976 | tf_op jit(solution)/shard_map/all_gather | solution.py:32
  12.8 249.6 %all-gather.5.cloned.1.call-start = ((), (), s32[]{:S(2)}) async-start(), calls=%async_computation.5 | async-start | bytes 33841152 | tf_op jit(solution)/shard_map/all_gather | solution.py:43
  56.0 10.3 %copy-start.3 = (bf16[8,41472]{1,0:T(8,128)(2,1)S(1)}, bf16[8,41472]{1,0:T(8,128)(2,1)}, u32[]{:S(2)}) copy-start(bf16[8,41472]{1,0:T(8,128)(2,1)} %get-tuple-element.52) | copy-start | bytes 1990660
  63.6 7.9 %copy-start.6 = (bf16[1152,72]{0,1:T(8,128)(2,1)S(1)}, bf16[1152,72]{0,1:T(8,128)(2,1)}, u32[]{:S(2)}) copy-start(bf16[1152,72]{0,1:T(8,128)(2,1)} %copy.82) | copy-start | bytes 497668
  71.5 2.7 copy-start.20
  71.6 3.0 copy-start.15
  71.6 3.0 copy-start.17
  74.2 3.2 copy-start.7
  77.7 11.7 %copy-start.14 = (f32[1,32,256]{2,1,0:T(8,128)S(1)}, f32[1,32,256]{2,1,0:T(8,128)}, u32[]{:S(2)}) copy-start(f32[1,32,256]{2,1,0:T(8,128)} %param.18) | copy-start | bytes 98308
  80.9 8.4 %all-to-all-start.2 = ((bf16[8,2,1152]{2,1,0:T(2,128)(2,1)}), bf16[8,2,1152]{2,1,0:T(2,128)(2,1)S(1)}, u32[]{:S(2)}, u32[]{:S(2)}) async-start(bf16[8,2,1152]{2,1,0:T(2,128)(2,1)} %all_to_all.44), calls=%async_computation.2 | async-start | bytes 73728 | tf_op jit(solution)/shard_map/all_to_all | solution.py:196
  87.5 29.4 %copy-start.9 = (bf16[16,1152]{1,0:T(8,128)(2,1)S(1)}, bf16[16,1152]{1,0:T(8,128)(2,1)}, u32[]{:S(2)}) copy-start(bf16[16,1152]{1,0:T(8,128)(2,1)} %param.26) | copy-start | bytes 110596
  90.0 10.6 %all-to-all-start = ((f32[8,1,32,256]{3,2,1,0:T(8,128)}), f32[8,1,32,256]{3,2,1,0:T(8,128)S(1)}, u32[]{:S(2)}, u32[]{:S(2)}) async-start(f32[8,1,32,256]{3,2,1,0:T(8,128)} %broadcast_in_dim.44), calls=%async_computation | async-start | bytes 524288 | tf_op jit(solution)/shard_map/all_to_all | solution.py:23
  100.7 17.2 %copy-start.4 = (f32[8,1,32,256]{3,2,1,0:T(8,128)}, f32[8,1,32,256]{3,2,1,0:T(8,128)S(1)}, u32[]{:S(2)}) copy-start(f32[8,1,32,256]{3,2,1,0:T(8,128)S(1)} %all-to-all-done) | copy-start | bytes 786436
  103.3 13.2 %all-to-all-start.1 = ((bf16[16,2,256]{2,1,0:T(2,128)(2,1)}), bf16[16,2,256]{2,1,0:T(2,128)(2,1)S(1)}, u32[]{:S(2)}, u32[]{:S(2)}) async-start(bf16[16,2,256]{2,1,0:T(2,128)(2,1)} %reshape.344), calls=%async_computation.1 | async-start | bytes 32768 | tf_op jit(solution)/shard_map/all_to_all | solution.py:179
  117.4 1.5 copy-start.2
  285.9 1.3 copy-start.18
  287.3 1.0 copy-start.19
  292.3 1.3 copy-start.18
  293.6 1.0 copy-start.19
  361.4 16.3 %copy-start.16 = (s32[32,2]{0,1:T(2,128)S(1)}, s32[32,2]{0,1:T(2,128)}, u32[]{:S(2)}) copy-start(s32[32,2]{0,1:T(2,128)} %get-tuple-element.73) | copy-start | bytes 772
  361.4 16.3 %copy-start.5 = (f32[8,1,32,256]{3,2,1,0:T(8,128)S(1)}, f32[8,1,32,256]{3,2,1,0:T(8,128)}, u32[]{:S(2)}) copy-start(f32[8,1,32,256]{3,2,1,0:T(8,128)} %copy-done.4) | copy-start | bytes 786436
  361.4 23.5 %copy-start.1 = (bf16[1152,1152]{1,0:T(8,128)(2,1)S(1)}, bf16[1152,1152]{1,0:T(8,128)(2,1)}, u32[]{:S(2)}) copy-start(bf16[1152,1152]{1,0:T(8,128)(2,1)} %param.25) | copy-start | bytes 7962628
  371.2 13.0 %all-to-all-start.4 = ((f32[8,1,32,256]{3,2,1,0:T(8,128)}), f32[8,1,32,256]{3,2,1,0:T(8,128)S(1)}, u32[]{:S(2)}, u32[]{:S(2)}) async-start(f32[8,1,32,256]{3,2,1,0:T(8,128)} %broadcast_in_dim.85), calls=%async_computation.4 | async-start | bytes 524288 | tf_op jit(solution)/shard_map/all_to_all | solution.py:23
  (5 other events, 3.6 us)
Sparse Core Ops, SparseCore 0:
  12.9 34.7 all-gather.6
  74.4 187.9 all-gather.4
where the time goes:
time: 400 us; the launch traced here: 392 us
  waiting for transfers between devices  196 us (49%)
  local copies, waits for them, and re-layouts  67.7 us (17%)
  other arithmetic  42 us (10%)
  matrix products  39.2 us (10%)
  starting transfers between devices  21 us (5%)
  between operations  15 us (4%)
  blocking collectives  11.2 us (3%)
    all_gather x1, waiting for transfers between devices, gather_turned(): lax.all_gather(both, axis, axis=0, tiled=True)  143 us
    all_gather x1, waiting for transfers between devices, gather_packed(): lines, at, gathered = (lax.all_gather(line, axis), 0, [])  34.8 us
    unnamed x2, other arithmetic  23.3 us
    dot_general x1, matrix products, mlp_fn(): return jnp.dot(hidden_units, fc2_full, preferred_element_type=jnp.float32)  18.6 us
    unnamed x46, local copies, waits for them, and re-layouts  13.3 us
    all_to_all x1, blocking collectives, local(): lax.all_to_all(velocity_mid, 'batch', split_axis=2, concat_axis=1, tiled=...  11.2 us
    all_to_all x2, starting transfers between devices, from_everyone(): return lax.all_to_all(copies, axis, split_axis=0, concat_axis=0, tiled=True)  10.6 us
    all_to_all x2, waiting for transfers between devices, from_everyone(): return lax.all_to_all(copies, axis, split_axis=0, concat_axis=0, tiled=True)  10.3 us
  transfers between devices with their start and end apart: 6, of which 6 were waited for; matrix products, arithmetic and copies ran while one was open for 4% of the time, Pallas kernels for 0%

commit v1 on v0

v1 whole, which is shorter than its diff:
```python
import functools
import math

import jax
import jax.numpy as jnp
from jax import lax
from jax.experimental import pallas as pl
from jax.experimental.pallas import tpu as pltpu
from jax.sharding import PartitionSpec as P

D = 1152
HEADS = 16
FREQ = 256
GRID = 16
STEPS = 18
TOK = 512
BF = jnp.bfloat16
F32 = jnp.float32
MESH_ID = pl.DeviceIdType.MESH

GQ, GP, GF1, GG0, GG3 = 0, 1, 2, 3, 4
GK, GF0, GF2, GG1, GGR = 5, 6, 7, 8, 9
GV, GR, GF3, GG2 = 10, 11, 12, 13
GF = (GF0, GF1, GF2, GF3)
GG = (GG0, GG1, GG2, GG3)
ROUNDS = ((GQ, GK, GV), (GP, GF0, GR), (GF1, GF2, GF3), (GG0, GG1, GG2), (GG3, GGR))
GROUPS = (((0, 2), (5, 2), (10, 2)), ((2, 3), (7, 3), (12, 2)))
NT = (((1,), (1,)), ((), ()))


def part_of(tile):
    return 0 if tile < 5 else (1 if tile < 10 else 2)


def main_kernel(packed, patch, wpatch, mod, wfinal, out, w, xs, nb, att, hid, acc, *sems):
    psend, precv, tsend, trecv, dsend, drecv, lsem = sems
    tm = lax.axis_index("tm")
    ba = lax.axis_index("batch")
    x, c = tm // 2, tm % 2
    z, y = ba // 4, ba % 4
    coord = {"x": x, "y": y, "z": z}

    def device(axis, step):
        at = dict(coord)
        at[axis] = (at[axis] + step + 4) % 4
        return (at["x"] * 2 + c, at["z"] * 4 + at["y"])

    sibling = (x * 2 + 1 - c, ba)

    barrier = pltpu.get_barrier_semaphore()
    for axis in "xyz":
        for step in (1, -1):
            pl.semaphore_signal(barrier, inc=1, device_id=device(axis, step), device_id_type=MESH_ID)
    pl.semaphore_signal(barrier, inc=1, device_id=sibling, device_id_type=MESH_ID)
    pl.semaphore_wait(barrier, 7)

    ORDER = (("y", "z", "x"), ("x", "y", "z"), ("z", "x", "y"))

    def rows(v, start=0, size=72):
        return pl.ds(pl.multiple_of(72 * v + start, 8), size)

    def region(part, phase, g, v, half):
        if phase == 0:
            at = {**coord, ORDER[part][0]: v}
            r = rows(at["y"]) if half is None else (rows(at["y"], 0, 40) if half == 0 else rows(at["y"], 40, 32))
            return w.at[g, at["x"], c, at["z"], r, :]
        two = slice(None) if half is None else pl.ds(2 * half, 2)
        if phase == 1:
            if part == 0:
                return w.at[g, x, c, v, slice(None) if half is None else pl.ds(144 * half, 144), :]
            if part == 1:
                return w.at[g, two, c, z, rows(v), :]
            return w.at[g, v, c, two, rows(y), :]
        if part == 0:
            return w.at[g, v, c, two, :, :]
        if part == 1:
            return w.at[g, two, c, v, :, :]
        return w.at[g, two, c, :, rows(v), :]

    def copies(part, phase, g, send, recv, source=None):
        axis = ORDER[part][phase]
        v = coord[axis]
        up, down = (v + 1) % 4, (v + 3) % 4

        def remote(k):
            if k < 2:
                dst = region(part, phase, g, v, None)
                src = dst if source is None else source
            else:
                src = dst = region(part, phase, g, (down, up)[k - 2], k - 2)
            return pltpu.make_async_remote_copy(
                src_ref=src, dst_ref=dst, send_sem=send(k), recv_sem=recv(k),
                device_id=device(axis, (1, -1)[k % 2]), device_id_type=MESH_ID)

        return [functools.partial(remote, k) for k in range(4)]

    def arrival(part, phase, g, k, send, recv):
        axis = ORDER[part][phase]
        v = coord[axis]
        far = (v + 2) % 4
        ref = (
            region(part, phase, g, (v + 3) % 4, None), region(part, phase, g, (v + 1) % 4, None),
            region(part, phase, g, far, 0), region(part, phase, g, far, 1))[k]
        return pltpu.make_async_copy(ref, ref, recv(k))

    def pre_sems(group, part, phase):
        return (lambda k: psend.at[group, part, phase, k]), (lambda k: precv.at[group, part, phase, k])

    def pre(group, part, phase):
        g0, n = GROUPS[group][part]
        s, r = pre_sems(group, part, phase)
        source = packed.at[pl.ds(g0, n)] if phase == 0 else None
        return copies(part, phase, pl.ds(g0, n), s, r, source)

    def pre_wait(group, part, phase, ks):
        g0, n = GROUPS[group][part]
        s, r = pre_sems(group, part, phase)
        for k in ks:
            arrival(part, phase, pl.ds(g0, n), k, s, r).wait()

    def last(tile):
        return copies(part_of(tile), 2, tile, lambda k: tsend.at[tile, k], lambda k: trecv.at[tile, k])

    def last_wait(tile, ks):
        for k in ks:
            arrival(part_of(tile), 2, tile, k, lambda k: tsend.at[tile, k], lambda k: trecv.at[tile, k]).wait()

    def across(tile):
        return pltpu.make_async_remote_copy(
            src_ref=w.at[tile, :, c], dst_ref=w.at[tile, :, c], send_sem=dsend.at[tile],
            recv_sem=drecv.at[tile], device_id=sibling, device_id_type=MESH_ID)

    def across_wait(tile):
        ref = w.at[tile, :, 1 - c]
        pltpu.make_async_copy(ref, ref, drecv.at[tile]).wait()

    for group in (0, 1):
        for part in range(3):
            for cp in pre(group, part, 0)[:2]:
                cp().start()
    own = pltpu.make_async_copy(packed, w.at[:, x, c, z, rows(y), :], lsem)
    own.start()
    own.wait()
    for phase in (0, 1):
        for group in (0, 1):
            for part in range(3):
                pre_wait(group, part, phase, (0, 1))
                for cp in pre(group, part, phase)[2:]:
                    cp().start()
        for group in (0, 1):
            for part in range(3):
                pre_wait(group, part, phase, (2, 3))
                if phase == 0:
                    for cp in pre(group, part, 1)[:2]:
                        cp().start()
            if phase == 1 and group == 0:
                for r in (0, 1):
                    for tile in ROUNDS[r]:
                        for cp in last(tile)[:2]:
                            cp().start()

    def round_direct(r):
        for tile in ROUNDS[r]:
            last_wait(tile, (0, 1))
            for cp in last(tile)[2:]:
                cp().start()
        if r + 2 < len(ROUNDS):
            for tile in ROUNDS[r + 2]:
                for cp in last(tile)[:2]:
                    cp().start()

    def round_far(r):
        for tile in ROUNDS[r]:
            last_wait(tile, (2, 3))
            across(tile).start()

    def round_ready(r):
        for tile in ROUNDS[r]:
            across_wait(tile)

    def weights(tiles, t):
        return jnp.concatenate([w[g, t // 2, t % 2].reshape(D, 128) for g in tiles], axis=1)

    lane = lax.broadcasted_iota(jnp.int32, (GRID, D), 1)
    quarter = lane // (D // 4)
    omega = jnp.exp(-math.log(10000.0) * (lane - quarter * (D // 4)).astype(F32) / (D // 4))
    angle = lax.broadcasted_iota(jnp.int32, (GRID, D), 0).astype(F32) * omega
    table = jnp.where(quarter % 2 == 0, jnp.sin(angle), jnp.cos(angle))
    acc[0:GRID, :] = table
    lane_low = lane < D // 2
    wp = wpatch[...]

    def tokens_body(i, carry):
        r = i % GRID
        at = pl.ds(pl.multiple_of(i * GRID, GRID), GRID)
        position = jnp.where(lane_low, acc[0:GRID, :], acc[pl.ds(r, 1), :])
        xs[at, :] = jnp.dot(patch[at, :], wp, preferred_element_type=F32) + position
        return carry

    lax.fori_loop(0, TOK // GRID, tokens_body, 0)

    CH = 32

    def norm_rows(load, shift, scale, store):
        def body(i, carry):
            at = pl.ds(pl.multiple_of(i * CH, CH), CH)
            point = i // (TOK // CH // 2)
            v = load(at, point)
            mean = jnp.mean(v, axis=-1, keepdims=True)
            centred = v - mean
            var = jnp.mean(centred * centred, axis=-1, keepdims=True)
            normed = centred * lax.rsqrt(var + 1e-6)
            s = mod[pl.ds(point * 8 + scale, 1), :]
            h = mod[pl.ds(point * 8 + shift, 1), :]
            store(at, (normed * (1.0 + s) + h).astype(BF))
            return carry

        lax.fori_loop(0, TOK // CH, body, 0)

    def store_nb(at, v):
        nb[at, :] = v

    norm_rows(lambda at, point: xs[at, :], 0, 1, store_nb)

    round_direct(0)
    round_far(0)
    round_direct(1)
    round_far(1)
    round_ready(0)
    round_ready(1)

    l256 = lax.broadcasted_iota(jnp.int32, (256, 256), 1)

    def head_lanes(h, rem):
        tile = (l256 >= 64 * h) & (l256 < 64 * h + 64)
        tail = (l256 >= 128 + rem + 8 * h) & (l256 < 128 + rem + 8 * h + 8)
        return tile | tail

    scale = 1.0 / math.sqrt(72.0)

    def attn_body(t, carry):
        wqk = weights((GQ, GK), t)
        wvr = weights((GV, GR), t)

        def one_point(p, carry2):
            at = pl.ds(pl.multiple_of(p * 256, 256), 256)
            xn = nb[at, :]
            qk = jnp.dot(xn, wqk, preferred_element_type=F32)
            vr = jnp.dot(xn, wvr, preferred_element_type=F32)
            rem = vr[:, 128:]
            qq = jnp.concatenate([qk[:, :128], rem], axis=1).astype(BF)
            kk = jnp.concatenate([qk[:, 128:], pltpu.roll(rem, 112, 1)], axis=1).astype(BF)
            vv = jnp.concatenate([vr[:, :128], pltpu.roll(rem, 80, 1)], axis=1).astype(BF)
            outs = []
            for h in (0, 1):
                qh = jnp.where(head_lanes(h, 0), qq, jnp.zeros_like(qq))
                s = lax.dot_general(qh, kk, NT, preferred_element_type=F32)
                m = jnp.max(s, axis=-1, keepdims=True)
                e = jnp.exp((s - m) * scale)
                pb = (e / jnp.sum(e, axis=-1, keepdims=True)).astype(BF)
                outs.append(jnp.dot(pb, vv, preferred_element_type=F32))
            o = jnp.where(head_lanes(0, 112), outs[0], jnp.where(head_lanes(1, 112), outs[1], 0.0))
            att[t, at, :] = o.astype(BF)
            return carry2

        lax.fori_loop(0, 2, one_point, 0)
        return carry

    lax.fori_loop(0, 8, attn_body, 0)

    round_direct(2)
    round_far(2)
    round_ready(2)

    acc[...] = jnp.zeros_like(acc)

    def proj_body(t, carry):
        acc[...] += lax.dot_general(att[t], weights((GP, GR), t), NT, preferred_element_type=F32)
        return carry

    lax.fori_loop(0, 8, proj_body, 0)

    def load_mixed(at, point):
        v = xs[at, :] + mod[pl.ds(point * 8 + 2, 1), :] * acc[at, :]
        xs[at, :] = v
        return v

    norm_rows(load_mixed, 3, 4, store_nb)

    l128 = lax.broadcasted_iota(jnp.int32, (TOK, 128), 1)
    fc1_lanes = (l128 >= 48) & (l128 < 112)

    def fc1_body(t, carry):
        for i in range(2):
            h = jnp.dot(nb[...], weights(GF[2 * i : 2 * i + 2], t), preferred_element_type=F32)
            hid[t, :, 256 * i : 256 * i + 256] = jax.nn.gelu(h, approximate=True).astype(BF)
        h = jnp.dot(nb[...], weights((GR,), t), preferred_element_type=F32)
        hid[t, :, 512:640] = jnp.where(fc1_lanes, jax.nn.gelu(h, approximate=True), 0.0).astype(BF)
        return carry

    lax.fori_loop(0, 8, fc1_body, 0)

    round_direct(3)
    round_far(3)
    round_direct(4)
    round_far(4)
    round_ready(3)
    round_ready(4)

    acc[...] = jnp.zeros_like(acc)

    def fc2_body(t, carry):
        acc[...] += lax.dot_general(
            hid[t], weights((GG0, GG1, GG2, GG3, GGR), t), NT, preferred_element_type=F32)
        return carry

    lax.fori_loop(0, 8, fc2_body, 0)

    def load_residual(at, point):
        return xs[at, :] + mod[pl.ds(point * 8 + 5, 1), :] * acc[at, :]

    norm_rows(load_residual, 6, 7, store_nb)
    out[...] = jnp.dot(nb[...], wfinal[...], preferred_element_type=F32).astype(BF)

    for group in (0, 1):
        for part in range(3):
            for phase in (0, 1):
                for cp in pre(group, part, phase):
                    cp().wait_send()
    for tiles in ROUNDS:
        for tile in tiles:
            for cp in last(tile):
                cp().wait_send()
            across(tile).wait_send()


def denoise(packed, patch, w_patch, mod, w_final):
    vmem = pl.BlockSpec(memory_space=pltpu.VMEM)
    dma = pltpu.SemaphoreType.DMA
    return pl.pallas_call(
        main_kernel,
        out_shape=jax.ShapeDtypeStruct((TOK, 16), BF),
        in_specs=[vmem] * 5,
        out_specs=vmem,
        scratch_shapes=[
            pltpu.VMEM((14, 4, 2, 4, 288, 128), BF),
            pltpu.VMEM((TOK, D), F32),
            pltpu.VMEM((TOK, D), BF),
            pltpu.VMEM((8, TOK, 256), BF),
            pltpu.VMEM((8, TOK, 640), BF),
            pltpu.VMEM((TOK, D), F32),
            dma((2, 3, 2, 4)), dma((2, 3, 2, 4)),
            dma((14, 4)), dma((14, 4)),
            dma((14,)), dma((14,)),
            dma,
        ],
        compiler_params=pltpu.CompilerParams(
            collective_id=0, has_side_effects=True, vmem_limit_bytes=62 * 1024 * 1024),
        name="denoise",
    )(packed, patch, w_patch, mod, w_final)


def pack_weights(w_qkv, w_proj, w_fc1, w_fc2):
    heads = w_qkv.reshape(72, 2, 3, 72)
    main = [heads[:, :, j, :64].reshape(72, 128) for j in range(3)]
    rems = [heads[:, :, j, 64:].reshape(72, 16) for j in range(3)]
    proj = w_proj.T.reshape(72, 2, 72)
    fc2 = w_fc2.T
    tiles = [None] * 14
    tiles[GQ], tiles[GK], tiles[GV] = main
    tiles[GP] = proj[:, :, :64].reshape(72, 128)
    for i in range(4):
        tiles[GF[i]] = w_fc1[:, 128 * i : 128 * i + 128]
        tiles[GG[i]] = fc2[:, 128 * i : 128 * i + 128]
    tiles[GR] = jnp.concatenate(rems + [w_fc1[:, 512:], proj[:, :, 64:].reshape(72, 16)], axis=1)
    tiles[GGR] = jnp.pad(fc2[:, 512:], ((0, 0), (48, 16)))
    return jnp.stack(tiles)


def in_order(parts, dim):
    lengths = list(parts.shape[1:])
    lengths[dim] *= parts.shape[0]
    return jnp.moveaxis(parts, 0, dim).reshape(lengths)


def from_everyone(array, axis):
    copies = jnp.broadcast_to(array, (lax.axis_size(axis), *array.shape))
    return lax.all_to_all(copies, axis, split_axis=0, concat_axis=0, tiled=True)


def gathered_copies(array, axis, dim):
    return in_order(from_everyone(array, axis), dim)


def cond_activation(step_ids, class_ids, class_table, w_freq, w_time):
    half_freq = FREQ // 2
    freqs = jnp.exp(-math.log(10000.0) * jnp.arange(half_freq, dtype=jnp.float32) / half_freq)
    tvalue = 1000.0 * (1.0 - step_ids.astype(jnp.float32) / STEPS)
    angles = tvalue[:, None] * freqs[None, :]
    embedded = jnp.concatenate([jnp.cos(angles), jnp.sin(angles)], axis=1).astype(jnp.bfloat16)
    hidden_time = jax.nn.silu(jnp.dot(embedded, w_freq, preferred_element_type=jnp.float32)).astype(
        jnp.bfloat16
    )
    condition = jnp.dot(hidden_time, w_time, preferred_element_type=jnp.float32) + jnp.take(
        class_table, class_ids, axis=0
    ).astype(jnp.float32)
    return jax.nn.silu(condition).astype(jnp.bfloat16)


def local(
    latents,
    shifts,
    starts,
    labels,
    class_table,
    w_freq,
    w_time,
    w_ada,
    w_patch,
    w_qkv,
    w_proj,
    w_fc1,
    w_fc2,
    w_final,
):
    tm_count = lax.axis_size("tm")
    tm_index = lax.axis_index("tm")
    batch_index = lax.axis_index("batch")
    local_steps = latents.shape[0]
    window = local_steps * tm_count
    whole = gathered_copies(latents, "tm", 0)
    local_positions = tm_index * local_steps + jnp.arange(local_steps, dtype=jnp.int32)[:, None]
    source_rows = jnp.minimum(local_positions + shifts[None, :], window - 1)
    points = jnp.take_along_axis(whole, source_rows[:, :, None], axis=0)
    anchor = jnp.take_along_axis(whole, shifts[None, :, None], axis=0)[0]
    by_sample = lax.all_to_all(
        points.astype(jnp.bfloat16), "batch", split_axis=1, concat_axis=2, tiled=True
    )
    sample_count = by_sample.shape[1]
    lat_count = by_sample.shape[2]
    own_shifts = lax.dynamic_slice_in_dim(shifts, batch_index * sample_count, sample_count)
    own_starts = lax.dynamic_slice_in_dim(starts, batch_index * sample_count, sample_count)
    own_labels = lax.dynamic_slice_in_dim(labels, batch_index * sample_count, sample_count)
    window_positions = jnp.arange(window, dtype=jnp.int32)[:, None]
    step_ids = (own_starts + own_shifts)[None, :] + window_positions
    class_ids = jnp.broadcast_to(own_labels[None, :], step_ids.shape)
    activation = cond_activation(
        step_ids.reshape(-1), class_ids.reshape(-1), class_table, w_freq, w_time
    )
    own_columns = jnp.dot(activation, w_ada, preferred_element_type=jnp.float32).astype(
        jnp.bfloat16
    )
    modulation = lax.all_to_all(own_columns, "tm", split_axis=0, concat_axis=1, tiled=True)
    point_rows = by_sample.reshape(local_steps * sample_count, lat_count)
    point_count = point_rows.shape[0]
    packed = pack_weights(w_qkv, w_proj, w_fc1, w_fc2)
    patch = point_rows.reshape(TOK, 16)
    mod = modulation.astype(F32).reshape(16, D)
    velocity_mid = denoise(packed, patch, w_patch, mod, w_final)
    velocity_mid = velocity_mid.reshape(local_steps, sample_count, lat_count)
    velocity_out = lax.all_to_all(velocity_mid, "batch", split_axis=2, concat_axis=1, tiled=True)
    velocity_float = velocity_out.astype(jnp.float32)
    summed = jnp.cumsum(velocity_float, axis=0)
    running = jnp.concatenate([jnp.zeros_like(summed), summed[:-1]], axis=0)
    block_sum = jnp.sum(velocity_float, axis=0)
    block_sums = gathered_copies(block_sum[None], "tm", 0)
    lower_blocks = jnp.arange(tm_count, dtype=jnp.int32) < tm_index
    earlier_sum = jnp.sum(jnp.where(lower_blocks[:, None, None], block_sums, 0.0), axis=0)
    latents_out = anchor[None] + (earlier_sum[None] + running) * (1.0 / STEPS)
    return (latents_out, velocity_out)


def solution(mesh):
    placed = (
        P("tm", None, "batch"),
        P(),
        P(),
        P(),
        P(),
        P(),
        P(),
        P(None, "tm"),
        P(),
        P("batch", "tm"),
        P("tm", "batch"),
        P("batch", "tm"),
        P("tm", "batch"),
        P(),
    )
    return jax.shard_map(
        local,
        mesh=mesh,
        in_specs=placed,
        out_specs=(P("tm", None, "batch"), P("tm", None, "batch")),
        check_vma=False,
    )
```

time: 400 us -> 278 us (0.69); the launches traced: 392 us -> 276 us
  waiting for transfers between devices: 196 us -> 12.8 us
  Pallas kernels: 0 us -> 136 us
  matrix products: 39.2 us -> 3.39 us
  between operations: 15 us -> 0.86 us
  other arithmetic: 42 us -> 32.1 us
  local copies, waits for them, and re-layouts: 67.7 us -> 59.5 us
    all_gather x2 -> x0, waiting for transfers between devices: 178 us -> none  [the longest x1 143 us: gather_turned(): lax.all_gather(both, axis, axis=0, tiled=True)]
    pallas_call x0 -> x1, Pallas kernels: none -> 136 us  [denoise(): pl.pallas_call(main_kernel, out_shape=jax.ShapeDtypeStruct((TOK, 16), BF)...]
    dot_general x9 -> x0, matrix products: 36.4 us -> none  [the longest x1 18.6 us: mlp_fn(): return jnp.dot(hidden_units, fc2_full, preferred_element_type=jnp.float32)]
    unnamed x46 -> x28, local copies, waits for them, and re-layouts: 13.3 us -> 25.4 us
    reshape x9 -> x4, local copies, waits for them, and re-layouts: 16.5 us -> 5.17 us  [the longest x2 3.78 us: local(): velocity_mid = velocity_mid.reshape(local_steps, sample_count, lat_count)]
    sub x2 -> x0, other arithmetic: 6.23 us -> none  [one_point(): weights = jnp.exp(scores - peak)]
    while x9 -> x0, local copies, waits for them, and re-layouts: 6.03 us -> none
    all_to_all x2, waiting for transfers between devices: 10.3 us -> 5.02 us  [from_everyone(): return lax.all_to_all(copies, axis, split_axis=0, concat_axis=0, tiled=True)]
  transfers between devices with their start and end apart: 6 -> 4, of which waited for: 6 -> 3; matrix products, arithmetic and copies ran while one was open for 4% -> 20% of each run, Pallas kernels for 0% -> 0%
where the time goes in v1:
time: 278 us; the launch traced here: 276 us
  Pallas kernels  136 us (49%)
  local copies, waits for them, and re-layouts  59.5 us (21%)
  other arithmetic  32.1 us (12%)
  starting transfers between devices  21.7 us (8%)
  waiting for transfers between devices  12.8 us (5%)
  blocking collectives  10 us (4%)
  matrix products  3.39 us (1%)
    pallas_call x1, Pallas kernels, denoise(): pl.pallas_call(main_kernel, out_shape=jax.ShapeDtypeStruct((TOK, 16), BF)...  136 us
    unnamed x28, local copies, waits for them, and re-layouts  25.4 us
    unnamed x2, other arithmetic  24.3 us
    all_to_all x1, blocking collectives, local(): lax.all_to_all(velocity_mid, 'batch', split_axis=2, concat_axis=1, tiled=...  10 us
    all_to_all x2, starting transfers between devices, from_everyone(): return lax.all_to_all(copies, axis, split_axis=0, concat_axis=0, tiled=True)  9.15 us
    all_to_all x1, starting transfers between devices, local(): lax.all_to_all(points.astype(jnp.bfloat16), 'batch', split_axis=1, concat...  7.77 us
    another operation x5, local copies, waits for them, and re-layouts, pack_weights(): return jnp.stack(tiles)  5.79 us
    all_to_all x1, waiting for transfers between devices, local(): lax.all_to_all(points.astype(jnp.bfloat16), 'batch', split_axis=1, concat...  5.77 us
  transfers between devices with their start and end apart: 4, of which 3 were waited for; matrix products, arithmetic and copies ran while one was open for 20% of the time, Pallas kernels for 0%

profile of v1, /device:TPU:1, one launch (start us, length us, event | category | flops | bytes accessed | tf_op | source)
XLA Modules:
  0.0 275.9 jit_solution(17843877227601783690)
XLA Ops:
  0.7 1.6 broadcast_in_dim.56
  2.3 5.8 %all-to-all-start = ((f32[8,1,32,256]{3,2,1,0:T(8,128)}), f32[8,1,32,256]{3,2,1,0:T(8,128)S(1)}, u32[]{:S(2)}, u32[]{:S(2)}) async-start(f32[8,1,32,256]{3,2,1,0:T(8,128)} %broadcast_in_dim.56), calls=%async_computation | async-start | bytes 524288 | tf_op jit(solution)/shard_map/all_to_all | solution.py:388
  11.5 1.6 copy.85
  14.4 1.4 fusion.22
  26.2 1.5 copy.104
  29.9 1.4 copy.102
  43.2 1.4 constant_dynamic-update-slice_fusion.4
  48.8 3.3 %gather_fusion = bf16[16,1152]{1,0:T(8,128)(2,1)} fusion(bf16[1001,1152]{1,0:T(8,128)(2,1)} %param.20, s32[1024]{0:T(1024)} %pad_clamp_fusion), kind=kCustom, calls=%fused_computation.2 | custom fusion | bytes 73792 | tf_op jit(solution)/shard_map/jit(_take)/gather | solution.py:404
  53.6 2.6 convolution_convert_fusion
  56.8 1.6 copy.97.wfinal
  58.5 1.3 constant_dynamic-update-slice_fusion.packed
  59.8 4.8 %all-to-all-start.2 = ((bf16[8,2,1152]{2,1,0:T(2,128)(2,1)}), bf16[8,2,1152]{2,1,0:T(2,128)(2,1)S(1)}, u32[]{:S(2)}, u32[]{:S(2)}) async-start(bf16[8,2,1152]{2,1,0:T(2,128)(2,1)} %all_to_all.44), calls=%async_computation.2 | async-start | bytes 73728 | tf_op jit(solution)/shard_map/all_to_all | solution.py:453
  67.3 2.0 all-to-all-done.2
  69.3 7.8 %all-to-all-start.1 = ((bf16[16,2,256]{2,1,0:T(2,128)(2,1)}), bf16[16,2,256]{2,1,0:T(2,128)(2,1)S(1)}, u32[]{:S(2)}, u32[]{:S(2)}) async-start(bf16[16,2,256]{2,1,0:T(2,128)(2,1)} %reshape.217), calls=%async_computation.1 | async-start | bytes 32768 | tf_op jit(solution)/shard_map/all_to_all | solution.py:436
  77.8 5.8 %all-to-all-done.1 = bf16[16,2,256]{2,1,0:T(2,128)(2,1)S(1)} async-done(((bf16[16,2,256]{2,1,0:T(2,128)(2,1)}), bf16[16,2,256]{2,1,0:T(2,128)(2,1)S(1)}, u32[]{:S(2)}, u32[]{:S(2)}) %all-to-all-start.1) | async-done | bytes 16416 | tf_op jit(solution)/shard_map/all_to_all | solution.py:436
  84.5 135.6 %denoise.1 = bf16[512,16]{1,0:T(8,128)(2,1)} custom-call(bf16[14,72,128]{2,1,0:T(8,128)(2,1)} %constant_dynamic-update-slice_fusion.packed, bf16[512,16]{1,0:T(8,128)(2,1)} %reshape_reshape.3.patch, bf16[16,1152]{1,0:T(8,128)(2,1)} %wpatch.1, f32[16,1152]{1,0:T(8,128)} %bitcast.117, bf16[1152,16]{1,0:T(8,128)(2,1)} %copy.97.wfinal), custom_call_target="tpu_custom_call" | custom-call | tf_op jit(solution)/shard_map/denoise/pallas_call | solution.py:340
  221.1 2.7 copy.98
  223.9 23.6 %reduce.3 = bf16[4096,2]{1,0:T(8,128)(2,1)} reduce(bf16[4096,1,2]{2,1,0:T(2,128)(2,1)S(1)} %bitcast.111, bf16[]{:T(256)} %broadcast.196), dimensions={1}, to_apply=%bitcast.101.reduce_sub_computation | reduce | bytes 32770
  247.4 2.7 reshape.219
  250.1 10.0 %all_to_all.56 = bf16[16,2,256]{2,1,0:T(2,128)(2,1)S(1)} all-to-all(bf16[16,2,256]{2,1,0:T(2,128)(2,1)S(1)} %reshape.219), channel_id=1, replica_groups=mesh['tm'=8,'batch'=16] {'batch'}, dimensions={0} | all-to-all | bytes 32768 | tf_op jit(solution)/shard_map/all_to_all | solution.py:461
  260.1 2.4 reshape.220
  262.6 2.0 copy.99
  265.3 3.4 %all-to-all-start.4 = ((f32[8,1,32,256]{3,2,1,0:T(8,128)}), f32[8,1,32,256]{3,2,1,0:T(8,128)S(1)}, u32[]{:S(2)}, u32[]{:S(2)}) async-start(f32[8,1,32,256]{3,2,1,0:T(8,128)} %broadcast_in_dim.63), calls=%async_computation.4 | async-start | bytes 524288 | tf_op jit(solution)/shard_map/all_to_all | solution.py:388
  270.1 5.0 %all-to-all-done.4 = f32[8,1,32,256]{3,2,1,0:T(8,128)S(1)} async-done(((f32[8,1,32,256]{3,2,1,0:T(8,128)}), f32[8,1,32,256]{3,2,1,0:T(8,128)S(1)}, u32[]{:S(2)}, u32[]{:S(2)}) %all-to-all-start.4) | async-done | bytes 262176 | tf_op jit(solution)/shard_map/all_to_all | solution.py:388
  (77 shorter events, 43.7 us)
Async XLA Ops:
  0.6 52.1 %copy-start = (bf16[256,1152]{1,0:T(8,128)(2,1)S(1)}, bf16[256,1152]{1,0:T(8,128)(2,1)}, u32[]{:S(2)}) copy-start(bf16[256,1152]{1,0:T(8,128)(2,1)} %param.21) | copy-start | bytes 1769476
  0.6 53.0 %copy-start.1 = (bf16[1152,1152]{1,0:T(8,128)(2,1)S(1)}, bf16[1152,1152]{1,0:T(8,128)(2,1)}, u32[]{:S(2)}) copy-start(bf16[1152,1152]{1,0:T(8,128)(2,1)} %param.23) | copy-start | bytes 7962628
  2.3 57.5 %all-to-all-start = ((f32[8,1,32,256]{3,2,1,0:T(8,128)}), f32[8,1,32,256]{3,2,1,0:T(8,128)S(1)}, u32[]{:S(2)}, u32[]{:S(2)}) async-start(f32[8,1,32,256]{3,2,1,0:T(8,128)} %broadcast_in_dim.56), calls=%async_computation | async-start | bytes 524288 | tf_op jit(solution)/shard_map/all_to_all | solution.py:388
  53.6 11.7 %copy-start.3 = (pred[32]{0:T(512)(128)(4,1)S(1)}, pred[32]{0:T(512)(128)(4,1)}, u32[]{:S(2)}) copy-start(pred[32]{0:T(512)(128)(4,1)} %get-tuple-element.3) | copy-start | bytes 100
  59.8 9.5 %all-to-all-start.2 = ((bf16[8,2,1152]{2,1,0:T(2,128)(2,1)}), bf16[8,2,1152]{2,1,0:T(2,128)(2,1)S(1)}, u32[]{:S(2)}, u32[]{:S(2)}) async-start(bf16[8,2,1152]{2,1,0:T(2,128)(2,1)} %all_to_all.44), calls=%async_computation.2 | async-start | bytes 73728 | tf_op jit(solution)/shard_map/all_to_all | solution.py:453
  69.3 14.2 %all-to-all-start.1 = ((bf16[16,2,256]{2,1,0:T(2,128)(2,1)}), bf16[16,2,256]{2,1,0:T(2,128)(2,1)S(1)}, u32[]{:S(2)}, u32[]{:S(2)}) async-start(bf16[16,2,256]{2,1,0:T(2,128)(2,1)} %reshape.217), calls=%async_computation.1 | async-start | bytes 32768 | tf_op jit(solution)/shard_map/all_to_all | solution.py:436
  260.1 15.1 %copy-start.2 = (pred[32]{0:T(512)(128)(4,1)S(1)}, pred[32]{0:T(512)(128)(4,1)}, u32[]{:S(2)}) copy-start(pred[32]{0:T(512)(128)(4,1)} %get-tuple-element.15) | copy-start | bytes 100
  265.3 9.8 %all-to-all-start.4 = ((f32[8,1,32,256]{3,2,1,0:T(8,128)}), f32[8,1,32,256]{3,2,1,0:T(8,128)S(1)}, u32[]{:S(2)}, u32[]{:S(2)}) async-start(f32[8,1,32,256]{3,2,1,0:T(8,128)} %broadcast_in_dim.63), calls=%async_computation.4 | async-start | bytes 524288 | tf_op jit(solution)/shard_map/all_to_all | solution.py:388

commit v2 on v1

--- a/solution.py
+++ b/solution.py
@@ -11,6 +11,9 @@
 D = 1152
 HEADS = 16
 FREQ = 256
+NCLASS = 1001
+TM = 8
+BA = 16
 GRID = 16
 STEPS = 18
 TOK = 512
@@ -32,8 +35,14 @@
     return 0 if tile < 5 else (1 if tile < 10 else 2)
 
 
-def main_kernel(packed, patch, wpatch, mod, wfinal, out, w, xs, nb, att, hid, acc, *sems):
-    psend, precv, tsend, trecv, dsend, drecv, lsem = sems
+def main_kernel(
+    shifts, starts, labels, lat, wqkv, wproj, wfc1, wfc2, wpatch, wfinal, ctab, wfreq, wtime, wada,
+    lout, vout,
+    w, xs, nb, att, hid, acc, packed, win, anchor, ptsend, ptrecv, modsend, modrecv, velsend, velrecv,
+    whole, velb, vall, vfreq, vtime, vctab, vada, csem, *sems,
+):
+    psend, precv, tsend, trecv, dsend, drecv, lsem = sems[:7]
+    latsem, ptsem, modsem, velsem, sumsem = [sems[7 + 2 * i : 9 + 2 * i] for i in range(5)]
     tm = lax.axis_index("tm")
     ba = lax.axis_index("batch")
     x, c = tm // 2, tm % 2
@@ -48,11 +57,10 @@
     sibling = (x * 2 + 1 - c, ba)
 
     barrier = pltpu.get_barrier_semaphore()
-    for axis in "xyz":
-        for step in (1, -1):
-            pl.semaphore_signal(barrier, inc=1, device_id=device(axis, step), device_id_type=MESH_ID)
-    pl.semaphore_signal(barrier, inc=1, device_id=sibling, device_id_type=MESH_ID)
-    pl.semaphore_wait(barrier, 7)
+    for k in range(1, TM):
+        pl.semaphore_signal(barrier, inc=1, device_id=((tm + k) % TM, ba), device_id_type=MESH_ID)
+    for k in range(1, BA):
+        pl.semaphore_signal(barrier, inc=1, device_id=(tm, (ba + k) % BA), device_id_type=MESH_ID)
 
     ORDER = (("y", "z", "x"), ("x", "y", "z"), ("z", "x", "y"))
 
@@ -134,6 +142,70 @@
         ref = w.at[tile, :, 1 - c]
         pltpu.make_async_copy(ref, ref, drecv.at[tile]).wait()
 
+    def to_tm(k, src, dst, sems):
+        return pltpu.make_async_remote_copy(
+            src_ref=src, dst_ref=dst, send_sem=sems[0].at[k], recv_sem=sems[1].at[k],
+            device_id=((tm + k) % TM, ba), device_id_type=MESH_ID)
+
+    def to_batch(k, src, dst, sems):
+        return pltpu.make_async_remote_copy(
+            src_ref=src, dst_ref=dst, send_sem=sems[0].at[k], recv_sem=sems[1].at[k],
+            device_id=(tm, (ba + k) % BA), device_id_type=MESH_ID)
+
+    def landed(ref, sem):
+        pltpu.make_async_copy(ref, ref, sem).wait()
+
+    lat_copy = lambda k: to_tm(k, lat, win.at[tm], latsem)
+    pts_copy = lambda k: to_batch(k, ptsend.at[(ba + k) % BA], ptrecv.at[ba], ptsem)
+    mod_copy = lambda k: to_tm(k, modsend.at[(tm + k) % TM], modrecv.at[tm], modsem)
+    vel_copy = lambda k: to_batch(k, velsend.at[(ba + k) % BA], velrecv.at[ba], velsem)
+    sum_copy = lambda k: to_tm(k, velb, vall.at[tm], sumsem)
+
+    conditioning = [
+        pltpu.make_async_copy(src, dst, csem.at[i])
+        for i, (src, dst) in enumerate(((wfreq, vfreq), (wtime, vtime), (ctab, vctab), (wada, vada)))
+    ]
+    for cp in conditioning:
+        cp.start()
+
+    def lanes_from(count, width, source):
+        k = lax.broadcasted_iota(jnp.int32, (count, width), 0)
+        n = lax.broadcasted_iota(jnp.int32, (count, width), 1)
+        return jnp.where(k == source(n), 1.0, 0.0).astype(BF)
+
+    def qkv_lane(n):
+        tile, lane = n // 128, n % 128
+        main = 216 * (lane // 64) + 72 * tile + lane % 64
+        rem = 216 * ((lane % 16) // 8) + 72 * (lane // 16) + 64 + lane % 8
+        return jnp.where(tile < 3, main, jnp.where(lane < 48, rem, -1))
+
+    def proj_lane(n):
+        lane = n % 128
+        main = 72 * (lane // 64) + lane % 64
+        rem = 72 * ((lane - 112) // 8) + 64 + lane % 8
+        return jnp.where(n < 128, main, jnp.where(lane >= 112, rem, -1))
+
+    def fc_lane(n):
+        return jnp.where((n >= 48) & (n < 112), n - 48, -1)
+
+    q4 = jnp.dot(wqkv[...], lanes_from(432, 512, qkv_lane), preferred_element_type=F32)
+    p2 = lax.dot_general(
+        wproj[...], lanes_from(144, 256, proj_lane), (((0,), (0,)), ((), ())), preferred_element_type=F32)
+    f1 = jnp.dot(wfc1[:, 512:576], lanes_from(64, 128, fc_lane), preferred_element_type=F32)
+    f2 = jnp.dot(wfc2[:, 512:576], lanes_from(64, 128, fc_lane), preferred_element_type=F32)
+    for i, g in enumerate((GQ, GK, GV)):
+        packed[g] = q4[:, 128 * i : 128 * i + 128].astype(BF)
+    packed[GR] = (q4[:, 384:] + p2[:, 128:] + f1).astype(BF)
+    packed[GP] = p2[:, :128].astype(BF)
+    packed[GGR] = f2.astype(BF)
+    for i in range(4):
+        packed[GF[i]] = wfc1[:, 128 * i : 128 * i + 128]
+        packed[GG[i]] = wfc2[:, 128 * i : 128 * i + 128]
+
+    pl.semaphore_wait(barrier, TM + BA - 2)
+    for k in range(1, TM):
+        lat_copy(k).start()
+
     for group in (0, 1):
         for part in range(3):
             for cp in pre(group, part, 0)[:2]:
@@ -141,7 +213,7 @@
     own = pltpu.make_async_copy(packed, w.at[:, x, c, z, rows(y), :], lsem)
     own.start()
     own.wait()
-    for phase in (0, 1):
+    def first_phases(phase):
         for group in (0, 1):
             for part in range(3):
                 pre_wait(group, part, phase, (0, 1))
@@ -181,24 +253,6 @@
     def weights(tiles, t):
         return jnp.concatenate([w[g, t // 2, t % 2].reshape(D, 128) for g in tiles], axis=1)
 
-    lane = lax.broadcasted_iota(jnp.int32, (GRID, D), 1)
-    quarter = lane // (D // 4)
-    omega = jnp.exp(-math.log(10000.0) * (lane - quarter * (D // 4)).astype(F32) / (D // 4))
-    angle = lax.broadcasted_iota(jnp.int32, (GRID, D), 0).astype(F32) * omega
-    table = jnp.where(quarter % 2 == 0, jnp.sin(angle), jnp.cos(angle))
-    acc[0:GRID, :] = table
-    lane_low = lane < D // 2
-    wp = wpatch[...]
-
-    def tokens_body(i, carry):
-        r = i % GRID
-        at = pl.ds(pl.multiple_of(i * GRID, GRID), GRID)
-        position = jnp.where(lane_low, acc[0:GRID, :], acc[pl.ds(r, 1), :])
-        xs[at, :] = jnp.dot(patch[at, :], wp, preferred_element_type=F32) + position
-        return carry
-
-    lax.fori_loop(0, TOK // GRID, tokens_body, 0)
-
     CH = 32
 
     def norm_rows(load, shift, scale, store):
@@ -210,8 +264,8 @@
             centred = v - mean
             var = jnp.mean(centred * centred, axis=-1, keepdims=True)
             normed = centred * lax.rsqrt(var + 1e-6)
-            s = mod[pl.ds(point * 8 + scale, 1), :]
-            h = mod[pl.ds(point * 8 + shift, 1), :]
+            s = modrecv[scale, pl.ds(point, 1), :]
+            h = modrecv[shift, pl.ds(point, 1), :]
             store(at, (normed * (1.0 + s) + h).astype(BF))
             return carry
 
@@ -220,6 +274,76 @@
     def store_nb(at, v):
         nb[at, :] = v
 
+    lane = lax.broadcasted_iota(jnp.int32, (GRID, D), 1)
+    quarter = lane // (D // 4)
+    omega = jnp.exp(-math.log(10000.0) * (lane - quarter * (D // 4)).astype(F32) / (D // 4))
+    angle = lax.broadcasted_iota(jnp.int32, (GRID, D), 0).astype(F32) * omega
+    acc[256 : 256 + GRID, :] = jnp.where(quarter % 2 == 0, jnp.sin(angle), jnp.cos(angle))
+
+    def position_body(r, carry):
+        at = pl.ds(pl.multiple_of(r * GRID, GRID), GRID)
+        acc[at, :] = jnp.where(lane < D // 2, acc[256 : 256 + GRID, :], acc[pl.ds(256 + r, 1), :])
+        return carry
+
+    lax.fori_loop(0, GRID, position_body, 0)
+
+    win[tm] = lat[...]
+    for k in range(1, TM):
+        landed(win.at[(tm + TM - k) % TM], latsem[1].at[k])
+    for s in range(32):
+        move = shifts[s]
+        source = jnp.minimum(tm + move, TM - 1)
+        ptsend[s // 2, s % 2 : s % 2 + 1, :] = win[source, s : s + 1, :]
+        anchor[s : s + 1, :] = win[move, s : s + 1, :]
+    ptrecv[ba] = ptsend[ba]
+
+    first_phases(0)
+    for k in range(1, BA):
+        pts_copy(k).start()
+
+    row = lax.broadcasted_iota(jnp.int32, (16, 128), 0)
+    base = jnp.where(
+        row % 2 == 0, starts[2 * ba] + shifts[2 * ba], starts[2 * ba + 1] + shifts[2 * ba + 1])
+    tvalue = 1000.0 * (1.0 - (base + row // 2).astype(F32) / STEPS)
+    half = FREQ // 2
+    freqs = jnp.exp(
+        -math.log(10000.0) * lax.broadcasted_iota(jnp.int32, (16, 128), 1).astype(F32) / half)
+    angles = tvalue * freqs
+    embedded = jnp.concatenate([jnp.cos(angles), jnp.sin(angles)], axis=1).astype(BF)
+    for cp in conditioning:
+        cp.wait()
+    hidden_time = jax.nn.silu(jnp.dot(embedded, vfreq[...], preferred_element_type=F32)).astype(BF)
+    which = jnp.where(
+        lax.broadcasted_iota(jnp.int32, (16, NCLASS), 0) % 2 == 0, labels[2 * ba], labels[2 * ba + 1])
+    one_hot = jnp.where(
+        lax.broadcasted_iota(jnp.int32, (16, NCLASS), 1) == which, 1.0, 0.0).astype(BF)
+    condition = jnp.dot(hidden_time, vtime[...], preferred_element_type=F32) + jnp.dot(
+        one_hot, vctab[...], preferred_element_type=F32)
+    activation = jax.nn.silu(condition).astype(BF)
+    own_columns = jnp.dot(activation, vada[...], preferred_element_type=F32).astype(BF).astype(F32)
+    for j in range(TM):
+        modsend[j] = own_columns[2 * j : 2 * j + 2, :]
+    modrecv[tm] = modsend[tm]
+
+    for k in range(1, BA):
+        landed(ptrecv.at[(ba + BA - k) % BA], ptsem[1].at[k])
+    for k in range(1, TM):
+        mod_copy(k).start()
+    own_patch = lax.broadcasted_iota(jnp.int32, (GRID, 256), 1) // 16 == lax.broadcasted_iota(
+        jnp.int32, (GRID, 256), 0)
+    for p in range(2):
+        for b in range(BA):
+            values = jnp.where(own_patch, ptrecv[b, p : p + 1, :], 0.0)
+            att[0, 256 * p + 16 * b : 256 * p + 16 * b + 16, :] = values.astype(BF)
+    wp = jnp.concatenate([wpatch[...]] * 16, axis=0)
+    for i in range(4):
+        at = slice(128 * i, 128 * i + 128)
+        position = acc[128 * (i % 2) : 128 * (i % 2) + 128, :]
+        xs[at, :] = jnp.dot(att[0, at, :], wp, preferred_element_type=F32) + position
+
+    first_phases(1)
+    for k in range(1, TM):
+        landed(modrecv.at[(tm + TM - k) % TM], modsem[1].at[k])
     norm_rows(lambda at, point: xs[at, :], 0, 1, store_nb)
 
     round_direct(0)
@@ -281,7 +405,7 @@
     lax.fori_loop(0, 8, proj_body, 0)
 
     def load_mixed(at, point):
-        v = xs[at, :] + mod[pl.ds(point * 8 + 2, 1), :] * acc[at, :]
+        v = xs[at, :] + modrecv[2, pl.ds(point, 1), :] * acc[at, :]
         xs[at, :] = v
         return v
 
@@ -317,10 +441,21 @@
     lax.fori_loop(0, 8, fc2_body, 0)
 
     def load_residual(at, point):
-        return xs[at, :] + mod[pl.ds(point * 8 + 5, 1), :] * acc[at, :]
+        return xs[at, :] + modrecv[5, pl.ds(point, 1), :] * acc[at, :]
 
     norm_rows(load_residual, 6, 7, store_nb)
-    out[...] = jnp.dot(nb[...], wfinal[...], preferred_element_type=F32).astype(BF)
+    wf = jnp.concatenate([wfinal[...]] * 16, axis=0)
+    v = lax.dot_general(nb[...], wf, NT, preferred_element_type=F32)
+    own_value = lax.broadcasted_iota(jnp.int32, (TOK, 256), 1) // 16 == lax.broadcasted_iota(
+        jnp.int32, (TOK, 256), 0) % 16
+    v = jnp.where(own_value, v, 0.0).astype(BF)
+    out_row = lax.broadcasted_iota(jnp.int32, (32, TOK), 0)
+    token = lax.broadcasted_iota(jnp.int32, (32, TOK), 1)
+    pick = (out_row % 2 == token // 256) & (out_row // 2 == (token % 256) // 16)
+    v = jnp.dot(jnp.where(pick, 1.0, 0.0).astype(BF), v, preferred_element_type=F32)
+    for b in range(BA):
+        velsend[b] = v[2 * b : 2 * b + 2, :]
+    velrecv[ba] = velsend[ba]
 
     for group in (0, 1):
         for part in range(3):
@@ -332,142 +467,85 @@
             for cp in last(tile):
                 cp().wait_send()
             across(tile).wait_send()
-
-
-def denoise(packed, patch, w_patch, mod, w_final):
+    for k in range(1, TM):
+        lat_copy(k).wait_send()
+        mod_copy(k).wait_send()
+    for k in range(1, BA):
+        pts_copy(k).wait_send()
+
+    for k in range(1, BA):
+        vel_copy(k).start()
+    for k in range(1, BA):
+        landed(velrecv.at[(ba + BA - k) % BA], velsem[1].at[k])
+    for b in range(BA):
+        whole[2 * b : 2 * b + 2, :] = velrecv[b]
+    velocity = whole[...]
+    velb[...] = velocity.astype(BF)
+    vout[0] = velocity.astype(BF)
+    vall[tm] = velocity.astype(BF)
+    for k in range(1, BA):
+        vel_copy(k).wait_send()
+
+    for k in range(1, TM):
+        sum_copy(k).start()
+    for k in range(1, TM):
+        landed(vall.at[(tm + TM - k) % TM], sumsem[1].at[k])
+    total = jnp.zeros((32, 256), F32)
+    for i in range(TM):
+        total = total + jnp.where(i < tm, vall[i].astype(F32), 0.0)
+    lout[0] = anchor[...] + total * (1.0 / STEPS)
+    for k in range(1, TM):
+        sum_copy(k).wait_send()
+
+
+def local(latents, shifts, starts, labels, class_table, w_freq, w_time, w_ada, w_patch, w_qkv, w_proj,
+          w_fc1, w_fc2, w_final):
     vmem = pl.BlockSpec(memory_space=pltpu.VMEM)
+    smem = pl.BlockSpec(memory_space=pltpu.SMEM)
+    hbm = pl.BlockSpec(memory_space=pl.ANY)
     dma = pltpu.SemaphoreType.DMA
+    vm = pltpu.VMEM
     return pl.pallas_call(
         main_kernel,
-        out_shape=jax.ShapeDtypeStruct((TOK, 16), BF),
-        in_specs=[vmem] * 5,
-        out_specs=vmem,
+        out_shape=(
+            jax.ShapeDtypeStruct((1, 32, 256), F32),
+            jax.ShapeDtypeStruct((1, 32, 256), BF),
+        ),
+        in_specs=[smem] * 3 + [vmem] * 7 + [hbm] * 4,
+        out_specs=(vmem, vmem),
         scratch_shapes=[
-            pltpu.VMEM((14, 4, 2, 4, 288, 128), BF),
-            pltpu.VMEM((TOK, D), F32),
-            pltpu.VMEM((TOK, D), BF),
-            pltpu.VMEM((8, TOK, 256), BF),
-            pltpu.VMEM((8, TOK, 640), BF),
-            pltpu.VMEM((TOK, D), F32),
+            vm((14, 4, 2, 4, 288, 128), BF),
+            vm((TOK, D), F32),
+            vm((TOK, D), BF),
+            vm((8, TOK, 256), BF),
+            vm((8, TOK, 640), BF),
+            vm((TOK, D), F32),
+            vm((14, 72, 128), BF),
+            vm((TM, 32, 256), F32),
+            vm((32, 256), F32),
+            vm((BA, 2, 256), F32), vm((BA, 2, 256), F32),
+            vm((TM, 2, D), F32), vm((TM, 2, D), F32),
+            vm((BA, 2, 256), F32), vm((BA, 2, 256), F32),
+            vm((32, 256), F32),
+            vm((32, 256), BF),
+            vm((TM, 32, 256), BF),
+            vm((FREQ, D), BF), vm((D, D), BF), vm((NCLASS, D), BF), vm((D, D), BF),
+            dma((4,)),
             dma((2, 3, 2, 4)), dma((2, 3, 2, 4)),
             dma((14, 4)), dma((14, 4)),
             dma((14,)), dma((14,)),
             dma,
+            dma((TM,)), dma((TM,)),
+            dma((BA,)), dma((BA,)),
+            dma((TM,)), dma((TM,)),
+            dma((BA,)), dma((BA,)),
+            dma((TM,)), dma((TM,)),
         ],
         compiler_params=pltpu.CompilerParams(
-            collective_id=0, has_side_effects=True, vmem_limit_bytes=62 * 1024 * 1024),
+            collective_id=0, has_side_effects=True, vmem_limit_bytes=63 * 1024 * 1024),
         name="denoise",
-    )(packed, patch, w_patch, mod, w_final)
-
-
-def pack_weights(w_qkv, w_proj, w_fc1, w_fc2):
-    heads = w_qkv.reshape(72, 2, 3, 72)
-    main = [heads[:, :, j, :64].reshape(72, 128) for j in range(3)]
-    rems = [heads[:, :, j, 64:].reshape(72, 16) for j in range(3)]
-    proj = w_proj.T.reshape(72, 2, 72)
-    fc2 = w_fc2.T
-    tiles = [None] * 14
-    tiles[GQ], tiles[GK], tiles[GV] = main
-    tiles[GP] = proj[:, :, :64].reshape(72, 128)
-    for i in range(4):
-        tiles[GF[i]] = w_fc1[:, 128 * i : 128 * i + 128]
-        tiles[GG[i]] = fc2[:, 128 * i : 128 * i + 128]
-    tiles[GR] = jnp.concatenate(rems + [w_fc1[:, 512:], proj[:, :, 64:].reshape(72, 16)], axis=1)
-    tiles[GGR] = jnp.pad(fc2[:, 512:], ((0, 0), (48, 16)))
-    return jnp.stack(tiles)
-
-
-def in_order(parts, dim):
-    lengths = list(parts.shape[1:])
-    lengths[dim] *= parts.shape[0]
-    return jnp.moveaxis(parts, 0, dim).reshape(lengths)
-
-
-def from_everyone(array, axis):
-    copies = jnp.broadcast_to(array, (lax.axis_size(axis), *array.shape))
-    return lax.all_to_all(copies, axis, split_axis=0, concat_axis=0, tiled=True)
-
-
-def gathered_copies(array, axis, dim):
-    return in_order(from_everyone(array, axis), dim)
-
-
-def cond_activation(step_ids, class_ids, class_table, w_freq, w_time):
-    half_freq = FREQ // 2
-    freqs = jnp.exp(-math.log(10000.0) * jnp.arange(half_freq, dtype=jnp.float32) / half_freq)
-    tvalue = 1000.0 * (1.0 - step_ids.astype(jnp.float32) / STEPS)
-    angles = tvalue[:, None] * freqs[None, :]
-    embedded = jnp.concatenate([jnp.cos(angles), jnp.sin(angles)], axis=1).astype(jnp.bfloat16)
-    hidden_time = jax.nn.silu(jnp.dot(embedded, w_freq, preferred_element_type=jnp.float32)).astype(
-        jnp.bfloat16
-    )
-    condition = jnp.dot(hidden_time, w_time, preferred_element_type=jnp.float32) + jnp.take(
-        class_table, class_ids, axis=0
-    ).astype(jnp.float32)
-    return jax.nn.silu(condition).astype(jnp.bfloat16)
-
-
-def local(
-    latents,
-    shifts,
-    starts,
-    labels,
-    class_table,
-    w_freq,
-    w_time,
-    w_ada,
-    w_patch,
-    w_qkv,
-    w_proj,
-    w_fc1,
-    w_fc2,
-    w_final,
-):
-    tm_count = lax.axis_size("tm")
-    tm_index = lax.axis_index("tm")
-    batch_index = lax.axis_index("batch")
-    local_steps = latents.shape[0]
-    window = local_steps * tm_count
-    whole = gathered_copies(latents, "tm", 0)
-    local_positions = tm_index * local_steps + jnp.arange(local_steps, dtype=jnp.int32)[:, None]
-    source_rows = jnp.minimum(local_positions + shifts[None, :], window - 1)
-    points = jnp.take_along_axis(whole, source_rows[:, :, None], axis=0)
-    anchor = jnp.take_along_axis(whole, shifts[None, :, None], axis=0)[0]
-    by_sample = lax.all_to_all(
-        points.astype(jnp.bfloat16), "batch", split_axis=1, concat_axis=2, tiled=True
-    )
-    sample_count = by_sample.shape[1]
-    lat_count = by_sample.shape[2]
-    own_shifts = lax.dynamic_slice_in_dim(shifts, batch_index * sample_count, sample_count)
-    own_starts = lax.dynamic_slice_in_dim(starts, batch_index * sample_count, sample_count)
-    own_labels = lax.dynamic_slice_in_dim(labels, batch_index * sample_count, sample_count)
-    window_positions = jnp.arange(window, dtype=jnp.int32)[:, None]
-    step_ids = (own_starts + own_shifts)[None, :] + window_positions
-    class_ids = jnp.broadcast_to(own_labels[None, :], step_ids.shape)
-    activation = cond_activation(
-        step_ids.reshape(-1), class_ids.reshape(-1), class_table, w_freq, w_time
-    )
-    own_columns = jnp.dot(activation, w_ada, preferred_element_type=jnp.float32).astype(
-        jnp.bfloat16
-    )
-    modulation = lax.all_to_all(own_columns, "tm", split_axis=0, concat_axis=1, tiled=True)
-    point_rows = by_sample.reshape(local_steps * sample_count, lat_count)
-    point_count = point_rows.shape[0]
-    packed = pack_weights(w_qkv, w_proj, w_fc1, w_fc2)
-    patch = point_rows.reshape(TOK, 16)
-    mod = modulation.astype(F32).reshape(16, D)
-    velocity_mid = denoise(packed, patch, w_patch, mod, w_final)
-    velocity_mid = velocity_mid.reshape(local_steps, sample_count, lat_count)
-    velocity_out = lax.all_to_all(velocity_mid, "batch", split_axis=2, concat_axis=1, tiled=True)
-    velocity_float = velocity_out.astype(jnp.float32)
-    summed = jnp.cumsum(velocity_float, axis=0)
-    running = jnp.concatenate([jnp.zeros_like(summed), summed[:-1]], axis=0)
-    block_sum = jnp.sum(velocity_float, axis=0)
-    block_sums = gathered_copies(block_sum[None], "tm", 0)
-    lower_blocks = jnp.arange(tm_count, dtype=jnp.int32) < tm_index
-    earlier_sum = jnp.sum(jnp.where(lower_blocks[:, None, None], block_sums, 0.0), axis=0)
-    latents_out = anchor[None] + (earlier_sum[None] + running) * (1.0 / STEPS)
-    return (latents_out, velocity_out)
+    )(shifts, starts, labels, latents.reshape(32, 256), w_qkv, w_proj, w_fc1, w_fc2.T, w_patch,
+      w_final.T, class_table, w_freq, w_time, w_ada)
 
 
 def solution(mesh):

time: 278 us -> 161 us (0.58)
  local copies, waits for them, and re-layouts: 59.5 us -> 2.7 us
  other arithmetic: 32.1 us -> 0 us
  starting transfers between devices: 21.7 us -> 0 us
  Pallas kernels: 136 us -> 157 us
  waiting for transfers between devices: 12.8 us -> 0 us
  blocking collectives: 10 us -> 0 us
  matrix products: 3.39 us -> 0 us
    unnamed x2 -> x0, other arithmetic: 24.3 us -> none
    unnamed x28 -> x2, local copies, waits for them, and re-layouts: 25.4 us -> 2.7 us
    all_to_all x4 -> x0, starting transfers between devices: 21.7 us -> none  [the longest x2 9.15 us: from_everyone(): return lax.all_to_all(copies, axis, split_axis=0, concat_axis=0, tiled=True)]
    pallas_call x1, Pallas kernels: 136 us -> 157 us  [local(): pl.pallas_call(main_kernel, out_shape=(jax.ShapeDtypeStruct((1, 32, 256),...]
    all_to_all x4 -> x0, waiting for transfers between devices: 12.8 us -> none  [the longest x1 5.77 us: local(): lax.all_to_all(points.astype(jnp.bfloat16), 'batch', split_axis=1, concat...]
    another operation x11 -> x0, local copies, waits for them, and re-layouts: 10 us -> none  [the longest x5 5.79 us: pack_weights(): return jnp.stack(tiles)]
    all_to_all x1 -> x0, blocking collectives: 10 us -> none  [local(): lax.all_to_all(velocity_mid, 'batch', split_axis=2, concat_axis=1, tiled=...]
    reshape x6 -> x0, local copies, waits for them, and re-layouts: 5.81 us -> none  [the longest x2 3.78 us: local(): velocity_mid = velocity_mid.reshape(local_steps, sample_count, lat_count)]
  transfers between devices with their start and end apart: 4 -> 0, of which waited for: 3 -> 0; matrix products, arithmetic and copies ran while one was open for 20% -> 0% of each run, Pallas kernels for 0% -> 0%
where the time goes in v2:
time: 161 us; the launch traced here: 160 us
  Pallas kernels  157 us (98%)
  local copies, waits for them, and re-layouts  2.7 us (2%)
    pallas_call x1, Pallas kernels, local(): pl.pallas_call(main_kernel, out_shape=(jax.ShapeDtypeStruct((1, 32, 256),...  157 us

profile of v2, /device:TPU:1, one launch (start us, length us, event | category | flops | bytes accessed | tf_op | source)
XLA Modules:
  0.0 160.4 jit_solution(3069534262563295794)
XLA Ops:
  0.6 157.0 %denoise.1 = (f32[1,32,256]{2,1,0:T(8,128)}, bf16[1,32,256]{2,1,0:T(8,128)(2,1)}) custom-call(s32[32]{0:T(128)} %shifts.1, s32[32]{0:T(128)} %starts.1, s32[32]{0:T(128)} %labels.1, f32[32,256]{1,0:T(8,128)} %bitcast.5, bf16[72,432]{1,0:T(8,128)(2,1)} %wqkv.1, bf16[144,72]{1,0:T(8,128)(2,1)} %wproj.1, bf16[72,576]{1,0:T(8,128)(2,1)} %wfc1.1, ...), custom_call_target="tpu_custom_call" | custom-call | tf_op jit(solution)/shard_map/denoise/pallas_call | solution.py:508
  157.7 1.4 copy.18
  159.0 1.3 copy.19
